TPU v7x, 32 devices: a whole 2x2x4 slice. The times are simulated.
32 devices in a mesh: groups: 2 (over y), seq: 4 (over z), head: 4 (over x, core).
Axes of the slice: x: 2, y: 2, z: 4, core: 2. Of those that a mesh axis runs over, the one named last changes fastest.
Arguments:
- residual: bfloat16 [1024, 2048], P(('groups', 'seq')), parts along dimension 0, may hold values from -6 to 6
- query_in: bfloat16 [1024, 2048], P(('groups', 'seq'), 'head'), parts along dimension 0, may hold values from -6 to 6
- key_in: bfloat16 [1024, 2048], P(('groups', 'seq'), 'head'), parts along dimension 0, may hold values from -6 to 6
- value_in: bfloat16 [1024, 4096], P(('groups', 'seq'), 'head'), parts along dimension 0, may hold values from -6 to 6
- gating_in: bfloat16 [1024, 4096], P(('groups', 'seq'), 'head'), parts along dimension 0, may hold values from -6 to 6
- beta_logit: float32 [1024, 32], P(('groups', 'seq'), 'head'), parts along dimension 0, may hold values from -12 to 2
- decay_logit: float32 [1024, 32], P(('groups', 'seq'), 'head'), parts along dimension 0, may hold values from -16 to 1
- seq_length: int32 [2], P('groups'), parts along dimension 0, may hold values from 256 to 512
- conv_query: float32 [4, 2048], P(None, 'head'), may hold values from -3 to 3
- conv_key: float32 [4, 2048], P(None, 'head'), may hold values from -3 to 3
- conv_value: float32 [4, 4096], P(None, 'head'), may hold values from -3 to 3
- decay_rate: float32 [32], P('head'), may hold values from 0.5 to 17
- norm_gain: float32 [128], replicated, may hold values from 0.1 to 1.9
- out_weight: bfloat16 [4096, 2048], P('head'), may hold values from -0.09375 to 0.09375
- attn_gain: float32 [2048], replicated, may hold values from 0.1 to 1.9
- query_weight: bfloat16 [2048, 8192], P('seq', 'head'), may hold values from -1 to 1
- key_value_weight: bfloat16 [2048, 1024], P('seq'), may hold values from -10 to 10
Outputs:
- hidden_out: bfloat16 [1024, 2048], P(('groups', 'seq')), parts along dimension 0
- attention_out: bfloat16 [1024, 4096], P(('groups', 'seq'), 'head'), parts along dimension 0
There are 2 independent parts, one for each index of `groups`. A program takes and returns all parts, laid end to end along the dimension named above; an argument that names none is the same for every part. Nothing has to cross between parts.
All inputs are finite; a program needn't handle non-finite values.
Results may differ from a plain program's by a relative error of at most 0.02.
The roundings to bfloat16 on the way count: a program that leaves them out, or rounds other values in their place, can miss the bound.
Values may be sent and summed in bfloat16 or wider, within the bound.
A program may use at most 128 MiB of HBM per device.

v0:
```python
import jax
import jax.numpy as jnp
from jax import lax
from jax.sharding import PartitionSpec as P

DK = 128
DV = 128
QUERY_HEADS = 16
KEY_VALUE_HEADS = 2
HEAD_WIDTH = 256
CONV = 4
SPAN = 64


EPSILON = 1e-06
NEGATIVE = -1e30


def shifted(shard, axis, by):
    count = lax.axis_size(axis)
    pairs = [(i, i + by) for i in range(count) if 0 <= i + by < count]
    return lax.ppermute(shard, axis, pairs)


def entering_2(shard, axis, combine, identity):
    count, mine = (lax.axis_size(axis), lax.axis_index(axis))
    everything = jax.tree.map(lambda part: lax.all_gather(part, axis), shard)
    start = jax.tree.map(
        lambda part, zero: jnp.broadcast_to(jnp.asarray(zero, part.dtype), part.shape),
        shard,
        identity,
    )

    def hop(k, before):
        reached = k < mine
        new = combine(before, jax.tree.map(lambda part: part[k], everything))
        return jax.tree.map(lambda a, b: jnp.where(reached, a, b), new, before)

    return lax.fori_loop(0, count, hop, start)


def conv_silu(inputs, tail_rows, kernel):
    joined = jnp.concatenate([tail_rows, inputs], 0).astype(jnp.float32)
    row_total = inputs.shape[0]
    summed = jnp.zeros((row_total, inputs.shape[1]), jnp.float32)
    for offset in range(CONV):
        summed = summed + kernel[offset] * joined[offset : offset + row_total]
    return jax.nn.silu(summed)


def unit_rows(tensor):
    return tensor / jnp.sqrt(jnp.sum(tensor * tensor, -1, keepdims=True) + EPSILON)


def rms_scaled(tensor, gain_vector):
    return tensor * lax.rsqrt(jnp.mean(tensor * tensor, -1, keepdims=True) + EPSILON) * gain_vector


def span_terms(queries, keyset, values, betas, log_decay):
    highest_index = lax.Precision.HIGHEST
    running_totals = jnp.cumsum(log_decay, -1)
    block_size = log_decay.shape[-1]
    order_ids = jnp.arange(block_size)
    inclusive = order_ids[:, None] >= order_ids[None, :]
    strict = order_ids[:, None] > order_ids[None, :]
    spread = running_totals[..., :, None] - running_totals[..., None, :]
    within = jnp.where(inclusive, jnp.exp(jnp.where(inclusive, spread, 0.0)), 0.0)
    key_gram = jnp.einsum("nhik,nhjk->nhij", keyset, keyset, precision=highest_index)
    lower_part = jnp.where(strict, betas[..., :, None] * within * key_gram, 0.0) + jnp.eye(
        block_size, dtype=jnp.float32
    )
    right_side = jnp.concatenate(
        [(betas * jnp.exp(running_totals))[..., None] * keyset, betas[..., None] * values], -1
    )
    solved = jax.scipy.linalg.solve_triangular(
        lower_part, right_side, lower=True, unit_diagonal=True
    )
    key_width = keyset.shape[-1]
    weights_w = solved[..., :key_width]
    updates = solved[..., key_width:]
    mixing = jnp.einsum("nhik,nhjk->nhij", queries, keyset, precision=highest_index) * within
    local_out = jnp.einsum("nhij,nhjv->nhiv", mixing, updates, precision=highest_index)
    carry_map = jnp.exp(running_totals)[..., None] * queries - jnp.einsum(
        "nhij,nhjk->nhik", mixing, weights_w, precision=highest_index
    )
    stop_boundary = jnp.exp(running_totals[..., -1:] - running_totals)[..., None] * keyset
    transition = jnp.exp(running_totals[..., -1])[..., None, None] * jnp.eye(
        key_width, dtype=jnp.float32
    ) - jnp.einsum("nhjk,nhjl->nhkl", stop_boundary, weights_w, precision=highest_index)
    injected = jnp.einsum("nhjk,nhjv->nhkv", stop_boundary, updates, precision=highest_index)
    return (local_out, carry_map, transition, injected)


def compose_pair(earlier_rows, later_rows):
    highest_index = lax.Precision.HIGHEST
    return (
        jnp.einsum("hkl,hlm->hkm", later_rows[0], earlier_rows[0], precision=highest_index),
        jnp.einsum("auf,afi->aui", later_rows[0], earlier_rows[1], precision=highest_index)
        + later_rows[1],
    )


def shards(
    residual,
    query_in,
    key_in,
    value_in,
    gating_in,
    beta_logit,
    decay_logit,
    seq_length,
    conv_query,
    conv_key,
    conv_value,
    decay_rate,
    norm_gain,
    out_weight,
    attn_gain,
    query_weight,
    key_value_weight,
):
    highest_index = lax.Precision.HIGHEST
    row_count = residual.shape[0]
    seq_rank = lax.axis_index("seq")
    positions = seq_rank * row_count + jnp.arange(row_count, dtype=jnp.int32)
    length_now = seq_length[0]
    alive_mask = (positions < length_now).astype(jnp.float32)
    rim_start = row_count - CONV + 1
    tails = shifted((query_in[rim_start:], key_in[rim_start:], value_in[rim_start:]), "seq", 1)
    key_heads = query_in.shape[1] // DK
    value_heads = value_in.shape[1] // DV
    queries = unit_rows(
        conv_silu(query_in, tails[0], conv_query).reshape(row_count, key_heads, DK)
    ) * DK ** (-0.5)
    keyset = unit_rows(conv_silu(key_in, tails[1], conv_key).reshape(row_count, key_heads, DK))
    values = conv_silu(value_in, tails[2], conv_value).reshape(row_count, value_heads, DV)
    queries = jnp.repeat(queries, value_heads // key_heads, axis=1)
    keyset = jnp.repeat(keyset, value_heads // key_heads, axis=1)
    betas = jax.nn.sigmoid(beta_logit) * alive_mask[:, None]
    log_decay = -decay_rate[None, :] * jax.nn.softplus(decay_logit) * alive_mask[:, None]
    span_count = row_count // SPAN

    def to_spans(tensor):
        return tensor.reshape(span_count, SPAN, value_heads, tensor.shape[2]).transpose(0, 2, 1, 3)

    local_out, carry_map, transition, injected = span_terms(
        to_spans(queries),
        to_spans(keyset),
        to_spans(values),
        betas.reshape(span_count, SPAN, value_heads).transpose(0, 2, 1),
        log_decay.reshape(span_count, SPAN, value_heads).transpose(0, 2, 1),
    )
    identity_map = jnp.broadcast_to(jnp.eye(DK, dtype=jnp.float32), (value_heads, DK, DK))
    empty_state = jnp.zeros((value_heads, DK, DV), jnp.float32)

    def compose_spans(running, pair_now):
        return (compose_pair(running, pair_now), running)

    device_pair, prefix_pair = lax.scan(
        compose_spans, (identity_map, empty_state), (transition, injected)
    )
    entering = entering_2(device_pair, "seq", compose_pair, (identity_map, empty_state))[1]
    span_states = (
        jnp.einsum("nhkl,hlv->nhkv", prefix_pair[0], entering, precision=highest_index)
        + prefix_pair[1]
    )
    outputs = local_out + jnp.einsum(
        "nhik,nhkv->nhiv", carry_map, span_states, precision=highest_index
    )
    outputs = outputs.transpose(0, 2, 1, 3).reshape(row_count, value_heads, DV)
    gating = gating_in.astype(jnp.float32).reshape(row_count, value_heads, DV)
    gated = (
        (rms_scaled(outputs, norm_gain) * jax.nn.silu(gating))
        .astype(jnp.bfloat16)
        .reshape(row_count, value_heads * DV)
    )
    summed = lax.psum(jnp.dot(gated, out_weight, preferred_element_type=jnp.float32), "head")
    hidden_out = (residual.astype(jnp.float32) + summed).astype(jnp.bfloat16)
    normalized = rms_scaled(hidden_out.astype(jnp.float32), attn_gain).astype(jnp.bfloat16)
    attention_channel_id = lax.axis_index("head")
    query_head_rows = query_weight.shape[1] // (2 * HEAD_WIDTH)
    key_value_head = attention_channel_id * query_head_rows // (QUERY_HEADS // KEY_VALUE_HEADS)
    key_start = key_value_head * HEAD_WIDTH
    value_offset = (KEY_VALUE_HEADS + key_value_head) * HEAD_WIDTH
    picked = jnp.concatenate(
        [
            lax.dynamic_slice_in_dim(key_value_weight, key_start, HEAD_WIDTH, 1),
            lax.dynamic_slice_in_dim(key_value_weight, value_offset, HEAD_WIDTH, 1),
        ],
        1,
    )
    query_proj = jnp.dot(
        normalized,
        lax.all_gather(query_weight, "seq", axis=0, tiled=True),
        preferred_element_type=jnp.float32,
    )
    kv_proj = jnp.dot(
        normalized,
        lax.all_gather(picked, "seq", axis=0, tiled=True),
        preferred_element_type=jnp.float32,
    )
    key_rows = kv_proj[:, :HEAD_WIDTH].astype(jnp.bfloat16)
    value_rows = kv_proj[:, HEAD_WIDTH:].astype(jnp.bfloat16)
    query_proj = query_proj.reshape(row_count, query_head_rows, 2, HEAD_WIDTH)
    queries_att = query_proj[:, :, 0].astype(jnp.bfloat16)
    gating_att = query_proj[:, :, 1]
    half_rows = row_count // 2
    blocks = (queries_att[:half_rows], queries_att[half_rows:])
    block_positions = (positions[:half_rows], positions[half_rows:])
    start_state = (
        jnp.full((query_head_rows, half_rows), NEGATIVE, jnp.float32),
        jnp.zeros((query_head_rows, half_rows), jnp.float32),
        jnp.zeros((query_head_rows, half_rows, HEAD_WIDTH), jnp.float32),
    )
    running = (start_state, start_state)
    offset = jnp.int32(0)
    key_piece = lax.all_gather(key_rows, "seq", axis=0, tiled=True)
    value_piece = lax.all_gather(value_rows, "seq", axis=0, tiled=True)
    key_positions = jnp.arange(key_piece.shape[0], dtype=jnp.int32)
    updated = []
    for block_index in range(2):
        block_queries = blocks[block_index]
        query_positions = block_positions[block_index]
        needed = jnp.logical_and(offset <= query_positions[-1], offset < length_now)

        def refresh(recurrent_state):
            peak, total, accum = recurrent_state
            scores = jnp.einsum(
                "qhd,kd->hqk", block_queries, key_piece, preferred_element_type=jnp.float32
            ) * HEAD_WIDTH ** (-0.5)
            visible = (key_positions[None, :] <= query_positions[:, None]) & (
                key_positions[None, :] < length_now
            )
            scores = jnp.where(visible[None], scores, NEGATIVE)
            new_peak = jnp.maximum(peak, jnp.max(scores, -1))
            weights = jnp.where(visible[None], jnp.exp(scores - new_peak[..., None]), 0.0)
            return (
                new_peak,
                jnp.sum(weights, -1),
                jnp.einsum(
                    "hqk,kd->hqd",
                    weights.astype(jnp.bfloat16),
                    value_piece,
                    preferred_element_type=jnp.float32,
                ),
            )

        updated.append(
            lax.cond(needed, refresh, lambda recurrent_state: recurrent_state, running[block_index])
        )
    finished = tuple(updated)
    results = [
        (recurrent_state[2] / recurrent_state[1][..., None]).transpose(1, 0, 2)
        for recurrent_state in finished
    ]
    attended = jnp.concatenate(results, 0)
    attention_out = (
        (attended * jax.nn.sigmoid(gating_att))
        .astype(jnp.bfloat16)
        .reshape(row_count, query_head_rows * HEAD_WIDTH)
    )
    return (hidden_out, attention_out)


def solution(mesh):
    placed = (
        P(("groups", "seq"), None),
        P(("groups", "seq"), "head"),
        P(("groups", "seq"), "head"),
        P(("groups", "seq"), "head"),
        P(("groups", "seq"), "head"),
        P(("groups", "seq"), "head"),
        P(("groups", "seq"), "head"),
        P("groups"),
        P(None, "head"),
        P(None, "head"),
        P(None, "head"),
        P("head"),
        P(),
        P("head", None),
        P(),
        P("seq", "head"),
        P("seq", None),
    )
    return jax.shard_map(
        shards,
        mesh=mesh,
        in_specs=placed,
        out_specs=(P(("groups", "seq"), None), P(("groups", "seq"), "head")),
        check_vma=False,
    )
```

profile of v0, /device:TPU:0, one launch (start us, length us, event | category | flops | bytes accessed | tf_op | source)
XLA Modules:
  0.0 485.4 jit_solution(15018226329429035304)
XLA Ops:
  7.9 4.9 %collective-permute-start.1 = (bf16[3,512]{1,0:T(4,128)(2,1)S(1)}, bf16[3,512]{1,0:T(4,128)(2,1)S(1)}, u32[]{:S(2)}, u32[]{:S(2)}) collective-permute-start(bf16[3,512]{1,0:T(4,128)(2,1)S(1)} %slice.146), channel_id=1, source_target_pairs={{0,4},{4,8},{8,12},{1,5},{5,9},{9,13},{2,6},{6,10},{10,14},{3,7},{... | collective-permute-start | bytes 9224 | tf_op jit(solution)/shard_map/ppermute | solution.py:22
  13.6 3.5 collective-permute-start.2
  24.8 78.6 %custom-call.4 = f32[2,8,1,64,64]{3,4,2,1,0:T(8,128)S(1)} custom-call(f32[2,8,1,64,64]{4,3,2,1,0:T(8,128)S(1)} %fusion.51), custom_call_target="InvertDiagBlocksLowerTriangular" | custom-call | tf_op jit(solution)/shard_map/jit(_solve_triangular)/vmap(vmap())/triangular_solve | solution.py:75
  105.4 3.0 fusion.77
  108.4 2.0 convolution_subtract_fusion
  110.5 9.0 %while.31 = (s32[]{:T(128)}, f32[8,128,128]{2,1,0:T(8,128)S(1)}, f32[8,128,128]{2,1,0:T(8,128)S(1)}, f32[2,8,128,128]{3,2,1,0:T(8,128)}, f32[2,8,128,128]{2,3,1,...) while((s32[]{:T(128)}, f32[8,128,128]{2,1,0:T(8,128)S(1)}, ...), condition=%wide.region_4.5_spmd.clone, body=%wide.region_3.4_spmd.clone.sunk | while | flops 403046400 | bytes 14157960 | solution.py:159
  121.2 3.7 collective-permute-start
  129.5 36.0 %all-gather.11.cloned.1.call-done = f32[32,128,128]{2,1,0:T(8,128)} async-done(((f32[8,128,128]{2,1,0:T(8,128)}), f32[32,128,128]{2,1,0:T(8,128)}) %all-gather.11.cloned.1.call-update) | async-done | bytes 2097168 | tf_op jit(solution)/shard_map/all_gather | solution.py:27
  165.4 46.1 %all-gather.13.cloned.1.call-done = f32[32,128,128]{2,1,0:T(8,128)} async-done(((f32[8,128,128]{2,1,0:T(8,128)}), f32[32,128,128]{2,1,0:T(8,128)}) %all-gather.13.cloned.1.call-update) | async-done | bytes 2097168 | tf_op jit(solution)/shard_map/all_gather | solution.py:27
  211.5 7.9 %while.32 = (s32[]{:T(128)}, f32[8,128,128]{2,1,0:T(8,128)S(1)}, s32[]{:T(128)}, f32[4,8,128,128]{3,2,1,0:T(8,128)}, f32[4,8,128,128]{3,2,1,0:T(8,128)}, /*index=5*/s32[]{:T(128)}, s32[]{:T(128)}) while((s32[]{:T(128)}, f32[8,128,128]{2,1,0:T(8,128)S(1)}, s32[]{:T(128)}, f32[4,8,128,128]{3,2,1,0:T(8,128)}, ...), condition=%wide.region_6.7_spmd.clone, body=%wide.region_5.6_spmd.clone.sunk | while | flops 201850880 | bytes 3672671 | solution.py:39
  211.5 2.0 fusion.141
  213.6 1.9 fusion.141
  215.6 1.9 fusion.141
  217.5 1.9 fusion.141
  219.4 2.4 fusion.45
  221.8 2.2 multiply_reduce_fusion
  224.7 4.2 fusion.85
  232.5 31.6 %all-reduce.2.cloned.1.call-done = f32[128,2048]{1,0:T(8,128)} async-done(((f32[128,2048]{1,0:T(8,128)}), f32[128,2048]{1,0:T(8,128)}) %all-reduce.2.cloned.1.call-update) | async-done | bytes 1048592 | tf_op jit(solution)/shard_map/psum | solution.py:177
  265.6 46.1 %all-gather.9.cloned.1.call-done = bf16[2048,512]{1,0:T(8,128)(2,1)} async-done(((bf16[512,512]{1,0:T(8,128)(2,1)}), bf16[2048,512]{1,0:T(8,128)(2,1)}) %all-gather.9.cloned.1.call-update) | async-done | bytes 2097168 | tf_op jit(solution)/shard_map/all_gather | solution.py:199
  311.7 2.1 convolution_convert_fusion
  313.9 14.9 %all_gather.30 = bf16[512,256]{1,0:T(8,128)(2,1)S(1)} all-gather(bf16[128,256]{1,0:T(8,128)(2,1)S(1)} %get-tuple-element.284), channel_id=1, replica_groups=mesh['groups'=2,'seq'=4,'head'=4] {'seq'}, dimensions={0}, use_global_device_ids=true | all-gather | bytes 327680 | tf_op jit(solution)/shard_map/all_gather | solution.py:217
  328.8 24.9 %all_gather.31 = bf16[512,256]{1,0:T(8,128)(2,1)S(1)} all-gather(bf16[128,256]{1,0:T(8,128)(2,1)S(1)} %get-tuple-element.283), channel_id=1, replica_groups=mesh['groups'=2,'seq'=4,'head'=4] {'seq'}, dimensions={0}, use_global_device_ids=true | all-gather | bytes 327680 | tf_op jit(solution)/shard_map/all_gather | solution.py:218
  353.7 112.4 %all-gather.7.cloned.1.call-done = bf16[2048,2048]{1,0:T(8,128)(2,1)} async-done(((bf16[512,2048]{1,0:T(8,128)(2,1)}), bf16[2048,2048]{1,0:T(8,128)(2,1)}) %all-gather.7.cloned.1.call-update) | async-done | bytes 8388624 | tf_op jit(solution)/shard_map/all_gather | solution.py:194
  466.1 6.9 %fusion.99 = f32[128,2048]{0,1:T(8,128)S(1)} fusion(bf16[2048,2048]{1,0:T(8,128)(2,1)} %all-gather.7.cloned.1.call-done, bf16[128,2048]{1,0:T(8,128)(2,1)S(1)} %get-tuple-element.276, f32[2048]{0:T(1024)S(1)} %copy-done.15, f32[128]{0:T(128)S(1)} %add_rsqrt_fusion.1), kind=kOutput, calls=%fused_computation.153 | convolution fusion | flops 1074790400 | bytes 9970176 | tf_op jit(solution)/shard_map/dot_general | solution.py:192
  (162 shorter events, 38.8 us)
Async XLA Ops:
  7.2 117.8 %copy-start = (f32[128]{0:T(128)S(1)}, f32[128]{0:T(128)}, u32[]{:S(2)}) copy-start(f32[128]{0:T(128)} %param.37) | copy-start | bytes 1540
  7.2 158.3 %all-gather.11.cloned.1.call-start = ((), (), s32[]{:S(2)}) async-start(), calls=%async_computation.3 | async-start | bytes 2621440 | tf_op jit(solution)/shard_map/all_gather | solution.py:27
  7.9 14.0 %collective-permute-start.1 = (bf16[3,512]{1,0:T(4,128)(2,1)S(1)}, bf16[3,512]{1,0:T(4,128)(2,1)S(1)}, u32[]{:S(2)}, u32[]{:S(2)}) collective-permute-start(bf16[3,512]{1,0:T(4,128)(2,1)S(1)} %slice.146), channel_id=1, source_target_pairs={{0,4},{4,8},{8,12},{1,5},{5,9},{9,13},{2,6},{6,10},{10,14},{3,7},{... | collective-permute-start | bytes 9224 | tf_op jit(solution)/shard_map/ppermute | solution.py:22
  13.6 89.8 %collective-permute-start.2 = (bf16[3,1024]{1,0:T(4,128)(2,1)S(1)}, bf16[3,1024]{1,0:T(4,128)(2,1)S(1)}, u32[]{:S(2)}, u32[]{:S(2)}) collective-permute-start(bf16[3,1024]{1,0:T(4,128)(2,1)S(1)} %slice.155), channel_id=1, source_target_pairs={{0,4},{4,8},{8,12},{1,5},{5,9},{9,13},{2,6},{6,10},{10,14},{3,7},{... | collective-permute-start | bytes 18440 | tf_op jit(solution)/shard_map/ppermute | solution.py:22
  23.4 80.0 %copy-start.11 = (bf16[128,1024]{1,0:T(8,128)(2,1)S(1)}, bf16[128,1024]{1,0:T(8,128)(2,1)}, u32[]{:S(2)}) copy-start(bf16[128,1024]{1,0:T(8,128)(2,1)} %param.28) | copy-start | bytes 786436
  23.7 84.7 %copy-start.3 = (f32[128,4,2,128]{3,0,2,1:T(8,128)}, f32[128,4,2,128]{3,0,2,1:T(8,128)S(1)}, u32[]{:S(2)}) copy-start(f32[128,4,2,128]{3,0,2,1:T(8,128)S(1)} %broadcast_in_dim.123) | copy-start | bytes 1572868
  105.4 5.1 %copy-start.6 = (f32[2,8,64,256]{3,2,1,0:T(8,128)}, f32[2,8,64,256]{3,2,1,0:T(8,128)S(1)}, u32[]{:S(2)}) copy-start(f32[2,8,64,256]{3,2,1,0:T(8,128)S(1)} %fusion.55) | copy-start | bytes 3145732
  110.5 10.7 %copy-start.13 = (bf16[128,512]{1,0:T(8,128)(2,1)S(1)}, bf16[128,512]{1,0:T(8,128)(2,1)}, u32[]{:S(2)}) copy-start(bf16[128,512]{1,0:T(8,128)(2,1)} %param.26) | copy-start | bytes 393220
  110.5 14.4 %copy-start.14 = (f32[4,512]{1,0:T(4,128)S(1)}, f32[4,512]{1,0:T(4,128)}, u32[]{:S(2)}) copy-start(f32[4,512]{1,0:T(4,128)} %param.33) | copy-start | bytes 24580
  110.6 1.3 copy-start.5
  115.1 1.2 copy-start.5
  120.4 91.1 %all-gather.13.cloned.1.call-start = ((), (), s32[]{:S(2)}) async-start(), calls=%async_computation.4 | async-start | bytes 2621440 | tf_op jit(solution)/shard_map/all_gather | solution.py:27
  121.2 143.0 %all-reduce.2.cloned.1.call-start = ((), (), s32[]{:S(2)}) async-start(), calls=%async_computation | async-start | bytes 2097152 | tf_op jit(solution)/shard_map/psum | solution.py:177
  121.2 4.8 collective-permute-start
  126.1 1.1 copy-start.4
  126.4 1.8 copy-start.7
  211.5 7.9 %copy-start.9 = (f32[2,8,128,128]{2,3,1,0:T(8,128)S(1)}, f32[2,8,128,128]{2,3,1,0:T(8,128)}, u32[]{:S(2)}) copy-start(f32[2,8,128,128]{2,3,1,0:T(8,128)} %get-tuple-element.188) | copy-start | bytes 3145732
  221.8 2.9 copy-start.16
  224.7 4.3 copy-start.12
  228.9 82.8 %all-gather.9.cloned.1.call-start = ((), (), s32[]{:S(2)}) async-start(), calls=%async_computation.2 | async-start | bytes 2621440 | tf_op jit(solution)/shard_map/all_gather | solution.py:199
  229.1 35.1 %copy-start.10 = (bf16[128,2048]{1,0:T(8,128)(2,1)S(1)}, bf16[128,2048]{1,0:T(8,128)(2,1)}, u32[]{:S(2)}) copy-start(bf16[128,2048]{1,0:T(8,128)(2,1)} %param.25) | copy-start | bytes 1572868
  230.0 81.7 %copy-start.15 = (f32[2048]{0:T(1024)S(1)}, f32[2048]{0:T(1024)}, u32[]{:S(2)}) copy-start(f32[2048]{0:T(1024)} %param.39) | copy-start | bytes 24580
  230.0 236.1 %all-gather.7.cloned.1.call-start = ((), (), s32[]{:S(2)}) async-start(), calls=%async_computation.1 | async-start | bytes 10485760 | tf_op jit(solution)/shard_map/all_gather | solution.py:194
  265.6 207.3 %copy-start.8 = (bf16[128,2048]{1,0:T(8,128)(2,1)}, bf16[128,2048]{1,0:T(8,128)(2,1)S(1)}, u32[]{:S(2)}) copy-start(bf16[128,2048]{1,0:T(8,128)(2,1)S(1)} %get-tuple-element.276) | copy-start | bytes 1572868
  (2 other events, 1.8 us)
Sparse Core Ops, SparseCore 0:
  120.5 44.8 all-gather.10
  167.0 44.4 all-gather.12
  229.0 35.0 all-reduce.1
  265.6 46.1 all-gather.8
  313.1 152.8 all-gather.6
where the time goes:
time: 486 us; the launch traced here: 485 us
  waiting for transfers between devices  274 us (56%)
  other arithmetic  88.6 us (18%)
  blocking collectives  39.8 us (8%)
  matrix products  38.7 us (8%)
  between operations  16.5 us (3%)
  local copies, waits for them, and re-layouts  14.8 us (3%)
  starting transfers between devices  12.3 us (3%)
    all_gather x1, waiting for transfers between devices, shards(): lax.all_gather(query_weight, 'seq', axis=0, tiled=True)  112 us
    all_gather x2, waiting for transfers between devices, entering_2(): everything = jax.tree.map(lambda part: lax.all_gather(part, axis), shard)  82 us
    another operation x3, other arithmetic, span_terms(): jax.scipy.linalg.solve_triangular(lower_part, right_side, lower=True, uni...  78.7 us
    all_gather x1, waiting for transfers between devices, shards(): lax.all_gather(picked, 'seq', axis=0, tiled=True)  46.1 us
    psum x1, waiting for transfers between devices, shards(): lax.psum(jnp.dot(gated, out_weight, preferred_element_type=jnp.float32),...  31.6 us
    all_gather x1, blocking collectives, shards(): value_piece = lax.all_gather(value_rows, 'seq', axis=0, tiled=True)  24.9 us
    all_gather x1, blocking collectives, shards(): key_piece = lax.all_gather(key_rows, 'seq', axis=0, tiled=True)  14.9 us
    ppermute x3, starting transfers between devices, shifted(): return lax.ppermute(shard, axis, pairs)  12.1 us
  transfers between devices with their start and end apart: 8, of which 6 were waited for; matrix products, arithmetic and copies ran while one was open for 19% of the time, Pallas kernels for 0%

commit v1 on v0

v1 whole, which is shorter than its diff:
```python
import functools

import jax
import jax.numpy as jnp
from jax import lax
from jax.experimental import pallas as pl
from jax.experimental.pallas import tpu as pltpu
from jax.sharding import PartitionSpec as P

DK = 128
DV = 128
QUERY_HEADS = 16
KEY_VALUE_HEADS = 2
HEAD_WIDTH = 256
CONV = 4
PAD = 8

EPSILON = 1e-06
NEGATIVE = -1e30
MESH = pl.DeviceIdType.MESH
HIGHEST = lax.Precision.HIGHEST


def mm(a, b, contract=((1,), (0,))):
    return lax.dot_general(
        a, b, (contract, ((), ())), precision=HIGHEST, preferred_element_type=jnp.float32
    )


def delta_kernel(
    count,
    q_ref,
    k_ref,
    v_ref,
    gate_ref,
    tail_ref,
    beta_ref,
    decay_ref,
    decay_t_ref,
    length_ref,
    cq_ref,
    ck_ref,
    cv_ref,
    rate_ref,
    rate_t_ref,
    gain_ref,
    out_ref,
    joined,
    enter,
    leave,
    send_sems,
    recv_sems,
):
    me = lax.axis_index("seq")
    rows = q_ref.shape[0]
    key_heads = q_ref.shape[1] // DK
    value_heads = v_ref.shape[1] // DV
    share = value_heads // key_heads
    barrier = pltpu.get_barrier_semaphore()

    for peer in (lax.rem(me + 1, count), lax.rem(me + count - 1, count)):
        pl.semaphore_signal(barrier, inc=1, device_id={"seq": peer}, device_id_type=MESH)
    pl.semaphore_wait(barrier, 2)

    @pl.when(me == 0)
    def _():
        enter[...] = jnp.zeros_like(enter)

    q_width = key_heads * DK
    joined[:PAD] = tail_ref[...]
    joined[PAD:, :q_width] = q_ref[...].astype(jnp.float32)
    joined[PAD:, q_width : 2 * q_width] = k_ref[...].astype(jnp.float32)
    joined[PAD:, 2 * q_width :] = v_ref[...].astype(jnp.float32)

    def conv(base, taps, h):
        column = base + h * DK
        total = jnp.zeros((rows, DK), jnp.float32)
        for j in range(CONV):
            first = PAD - CONV + 1 + j
            total = total + taps[j : j + 1, h * DK : (h + 1) * DK] * joined[
                first : first + rows, column : column + DK
            ]
        return total * jax.nn.sigmoid(total)

    def unit(x):
        return x / jnp.sqrt(jnp.sum(x * x, -1, keepdims=True) + EPSILON)

    length = length_ref[0]
    start = me * rows
    at_row = start + lax.broadcasted_iota(jnp.int32, (rows, value_heads), 0)
    alive = (at_row < length).astype(jnp.float32)
    at_column = start + lax.broadcasted_iota(jnp.int32, (value_heads, rows), 1)
    alive_t = (at_column < length).astype(jnp.float32)

    def softplus(x):
        return jnp.maximum(x, 0.0) + jnp.log1p(jnp.exp(-jnp.abs(x)))

    beta = jax.nn.sigmoid(beta_ref[...]) * alive
    step = -rate_ref[...] * softplus(decay_ref[...]) * alive
    step_t = -rate_t_ref[...] * softplus(decay_t_ref[...]) * alive_t
    row = lax.broadcasted_iota(jnp.int32, (rows, rows), 0)
    column = lax.broadcasted_iota(jnp.int32, (rows, rows), 1)
    inclusive = row >= column
    run = mm(inclusive.astype(jnp.float32), step)
    run_t = mm(step_t, (row <= column).astype(jnp.float32))
    growth = jnp.exp(run)
    ending = jnp.exp(run[rows - 1 : rows] - run)
    eye = (row == column).astype(jnp.float32)

    queries, keyset, grams, mixes = [], [], [], []
    for g in range(key_heads):
        q = unit(conv(0, cq_ref, g)) * DK ** (-0.5)
        k = unit(conv(q_width, ck_ref, g))
        queries.append(q)
        keyset.append(k)
        grams.append(mm(k, k, ((1,), (1,))))
        mixes.append(mm(q, k, ((1,), (1,))))

    within, lower, inverse = [], [], []
    for h in range(value_heads):
        spread = run[:, h : h + 1] - run_t[h : h + 1, :]
        w = jnp.where(inclusive, jnp.exp(jnp.where(inclusive, spread, 0.0)), 0.0)
        within.append(w)
        low = jnp.where(row > column, beta[:, h : h + 1] * w * grams[h // share], 0.0)
        lower.append(low)
        pair = (row // 2 == column // 2) & (row > column)
        inverse.append(eye - jnp.where(pair, low, 0.0))
    size = 2
    while size < rows:
        off = (row // (2 * size) == column // (2 * size)) & (row // size > column // size)
        half = [mm(jnp.where(off, low, 0.0), x) for low, x in zip(lower, inverse)]
        inverse = [x - mm(x, y) for x, y in zip(inverse, half)]
        size *= 2

    local, carry, transition, injected = [], [], [], []
    for h in range(value_heads):
        k = keyset[h // share]
        v = conv(2 * q_width, cv_ref, h)
        b = beta[:, h : h + 1]
        w = mm(inverse[h], b * growth[:, h : h + 1] * k)
        u = mm(inverse[h], b * v)
        mix = mixes[h // share] * within[h]
        stop = ending[:, h : h + 1] * k
        local.append(mm(mix, u))
        carry.append(growth[:, h : h + 1] * queries[h // share] - mm(mix, w))
        transition.append(
            growth[rows - 1 : rows, h : h + 1] * eye - mm(stop, w, ((0,), (0,)))
        )
        injected.append(mm(stop, u, ((0,), (0,))))

    copies = []
    for h in range(value_heads):
        copy = pltpu.make_async_remote_copy(
            src_ref=leave.at[h],
            dst_ref=enter.at[h],
            send_sem=send_sems.at[h],
            recv_sem=recv_sems.at[h],
            device_id={"seq": lax.rem(me + 1, count)},
            device_id_type=MESH,
        )
        copies.append(copy)

        @pl.when(me > 0)
        def _():
            copy.wait_recv()

        state = enter[h]
        leave[h] = mm(transition[h], state) + injected[h]
        o = local[h] + mm(carry[h], state)
        scaled = o * lax.rsqrt(jnp.mean(o * o, -1, keepdims=True) + EPSILON) * gain_ref[...]
        gate = gate_ref[:, h * DV : (h + 1) * DV].astype(jnp.float32)
        out_ref[:, h * DV : (h + 1) * DV] = (
            scaled * (gate * jax.nn.sigmoid(gate))
        ).astype(out_ref.dtype)

        @pl.when(me < count - 1)
        def _():
            copy.start()

    @pl.when(me < count - 1)
    def _():
        for copy in copies:
            copy.wait_send()


def delta(count, q, k, v, gate, beta_logit, decay_logit, seq_length, cq, ck, cv, rate, gain):
    rows, value_heads = beta_logit.shape
    width = q.shape[1] + k.shape[1] + v.shape[1]
    rim = rows - CONV + 1
    tail = jnp.concatenate([q[rim:], k[rim:], v[rim:]], 1)
    tail = shifted(tail, "seq", 1).astype(jnp.float32)
    tail = jnp.concatenate([jnp.zeros((PAD - CONV + 1, width), jnp.float32), tail], 0)
    vmem = pl.BlockSpec(memory_space=pltpu.VMEM)
    smem = pl.BlockSpec(memory_space=pltpu.SMEM)
    return pl.pallas_call(
        functools.partial(delta_kernel, count),
        out_shape=jax.ShapeDtypeStruct(gate.shape, jnp.bfloat16),
        in_specs=[vmem] * 8 + [smem] + [vmem] * 6,
        out_specs=vmem,
        scratch_shapes=[
            pltpu.VMEM((rows + PAD, width), jnp.float32),
            pltpu.VMEM((value_heads, DK, DV), jnp.float32),
            pltpu.VMEM((value_heads, DK, DV), jnp.float32),
            pltpu.SemaphoreType.DMA((value_heads,)),
            pltpu.SemaphoreType.DMA((value_heads,)),
        ],
        compiler_params=pltpu.CompilerParams(
            collective_id=0, has_side_effects=True, vmem_limit_bytes=32 * 2**20
        ),
        cost_estimate=pl.CostEstimate(
            flops=50_000_000_000, bytes_accessed=4_000_000, transcendentals=0
        ),
        name="delta_rule",
    )(
        q,
        k,
        v,
        gate,
        tail,
        beta_logit,
        decay_logit,
        decay_logit.T,
        seq_length,
        cq,
        ck,
        cv,
        rate[None, :],
        rate[:, None],
        gain[None, :],
    )


def shifted(shard, axis, by):
    count = lax.axis_size(axis)
    pairs = [(i, i + by) for i in range(count) if 0 <= i + by < count]
    return lax.ppermute(shard, axis, pairs)


def rms_scaled(tensor, gain_vector):
    return tensor * lax.rsqrt(jnp.mean(tensor * tensor, -1, keepdims=True) + EPSILON) * gain_vector


def pick(key_value_weight, query_weight):
    attention_channel_id = lax.axis_index("head")
    query_head_rows = query_weight.shape[1] // (2 * HEAD_WIDTH)
    key_value_head = attention_channel_id * query_head_rows // (QUERY_HEADS // KEY_VALUE_HEADS)
    key_start = key_value_head * HEAD_WIDTH
    value_offset = (KEY_VALUE_HEADS + key_value_head) * HEAD_WIDTH
    return jnp.concatenate(
        [
            lax.dynamic_slice_in_dim(key_value_weight, key_start, HEAD_WIDTH, 1),
            lax.dynamic_slice_in_dim(key_value_weight, value_offset, HEAD_WIDTH, 1),
        ],
        1,
    )


def shards(
    residual,
    query_in,
    key_in,
    value_in,
    gating_in,
    beta_logit,
    decay_logit,
    seq_length,
    conv_query,
    conv_key,
    conv_value,
    decay_rate,
    norm_gain,
    out_weight,
    attn_gain,
    query_weight,
    key_value_weight,
):
    row_count = residual.shape[0]
    seq_rank = lax.axis_index("seq")
    positions = seq_rank * row_count + jnp.arange(row_count, dtype=jnp.int32)
    length_now = seq_length[0]
    all_query_weight = lax.all_gather(query_weight, "seq", axis=0, tiled=True)
    picked = pick(key_value_weight, query_weight)
    all_picked = lax.all_gather(picked, "seq", axis=0, tiled=True)
    gated = delta(
        lax.axis_size("seq"),
        query_in,
        key_in,
        value_in,
        gating_in,
        beta_logit,
        decay_logit,
        seq_length,
        conv_query,
        conv_key,
        conv_value,
        decay_rate,
        norm_gain,
    )
    summed = lax.psum(jnp.dot(gated, out_weight, preferred_element_type=jnp.float32), "head")
    hidden_out = (residual.astype(jnp.float32) + summed).astype(jnp.bfloat16)
    normalized = rms_scaled(hidden_out.astype(jnp.float32), attn_gain).astype(jnp.bfloat16)
    query_head_rows = query_weight.shape[1] // (2 * HEAD_WIDTH)
    query_proj = jnp.dot(
        normalized,
        all_query_weight,
        preferred_element_type=jnp.float32,
    )
    kv_proj = jnp.dot(
        normalized,
        all_picked,
        preferred_element_type=jnp.float32,
    )
    query_proj = query_proj.reshape(row_count, query_head_rows, 2, HEAD_WIDTH)
    queries_att = query_proj[:, :, 0].astype(jnp.bfloat16)
    gating_att = query_proj[:, :, 1]
    half_rows = row_count // 2
    blocks = (queries_att[:half_rows], queries_att[half_rows:])
    block_positions = (positions[:half_rows], positions[half_rows:])
    start_state = (
        jnp.full((query_head_rows, half_rows), NEGATIVE, jnp.float32),
        jnp.zeros((query_head_rows, half_rows), jnp.float32),
        jnp.zeros((query_head_rows, half_rows, HEAD_WIDTH), jnp.float32),
    )
    running = (start_state, start_state)
    offset = jnp.int32(0)
    both = lax.all_gather(kv_proj.astype(jnp.bfloat16), "seq", axis=0, tiled=True)
    key_piece = both[:, :HEAD_WIDTH]
    value_piece = both[:, HEAD_WIDTH:]
    key_positions = jnp.arange(key_piece.shape[0], dtype=jnp.int32)
    updated = []
    for block_index in range(2):
        block_queries = blocks[block_index]
        query_positions = block_positions[block_index]
        needed = jnp.logical_and(offset <= query_positions[-1], offset < length_now)

        def refresh(recurrent_state):
            peak, _, _ = recurrent_state
            scores = jnp.einsum(
                "qhd,kd->hqk", block_queries, key_piece, preferred_element_type=jnp.float32
            ) * HEAD_WIDTH ** (-0.5)
            visible = (key_positions[None, :] <= query_positions[:, None]) & (
                key_positions[None, :] < length_now
            )
            scores = jnp.where(visible[None], scores, NEGATIVE)
            new_peak = jnp.maximum(peak, jnp.max(scores, -1))
            weights = jnp.where(visible[None], jnp.exp(scores - new_peak[..., None]), 0.0)
            return (
                new_peak,
                jnp.sum(weights, -1),
                jnp.einsum(
                    "hqk,kd->hqd",
                    weights.astype(jnp.bfloat16),
                    value_piece,
                    preferred_element_type=jnp.float32,
                ),
            )

        updated.append(
            lax.cond(needed, refresh, lambda recurrent_state: recurrent_state, running[block_index])
        )
    finished = tuple(updated)
    results = [
        (recurrent_state[2] / recurrent_state[1][..., None]).transpose(1, 0, 2)
        for recurrent_state in finished
    ]
    attended = jnp.concatenate(results, 0)
    attention_out = (
        (attended * jax.nn.sigmoid(gating_att))
        .astype(jnp.bfloat16)
        .reshape(row_count, query_head_rows * HEAD_WIDTH)
    )
    return (hidden_out, attention_out)


def solution(mesh):
    placed = (
        P(("groups", "seq"), None),
        P(("groups", "seq"), "head"),
        P(("groups", "seq"), "head"),
        P(("groups", "seq"), "head"),
        P(("groups", "seq"), "head"),
        P(("groups", "seq"), "head"),
        P(("groups", "seq"), "head"),
        P("groups"),
        P(None, "head"),
        P(None, "head"),
        P(None, "head"),
        P("head"),
        P(),
        P("head", None),
        P(),
        P("seq", "head"),
        P("seq", None),
    )

    return jax.shard_map(
        shards,
        mesh=mesh,
        in_specs=placed,
        out_specs=(P(("groups", "seq"), None), P(("groups", "seq"), "head")),
        check_vma=False,
    )
```

time: 486 us -> 281 us (0.58)
  waiting for transfers between devices: 274 us -> 184 us
  other arithmetic: 88.6 us -> 4.93 us
  matrix products: 38.7 us -> 11.9 us
  Pallas kernels: 0 us -> 23.6 us
  blocking collectives: 39.8 us -> 17.2 us
  starting transfers between devices: 12.3 us -> 5.08 us
    all_gather x4 -> x2, waiting for transfers between devices: 240 us -> 141 us  [the longest x1 132 us: shards(): all_query_weight = lax.all_gather(query_weight, 'seq', axis=0, tiled=True)]
    another operation x6 -> x0, other arithmetic: 79.1 us -> none  [the longest x3 78.7 us: span_terms(): jax.scipy.linalg.solve_triangular(lower_part, right_side, lower=True, uni...]
    pallas_call x0 -> x1, Pallas kernels: none -> 23.6 us  [delta(): pl.pallas_call(functools.partial(delta_kernel, count), out_shape=jax.Shap...]
    dot_general x18 -> x2, matrix products: 32.2 us -> 8.95 us  [the longest x1 6.86 us: shards(): jnp.dot(normalized, all_query_weight, preferred_element_type=jnp.float32)]
    all_gather x2 -> x1, blocking collectives: 39.8 us -> 17.2 us  [shards(): lax.all_gather(kv_proj.astype(jnp.bfloat16), 'seq', axis=0, tiled=True)]
    psum x1, waiting for transfers between devices: 31.6 us -> 42.4 us  [shards(): lax.psum(jnp.dot(gated, out_weight, preferred_element_type=jnp.float32),...]
    unnamed x35 -> x34, local copies, waits for them, and re-layouts: 2.44 us -> 10.5 us
    ppermute x3 -> x1, starting transfers between devices: 12.1 us -> 4.96 us  [shifted(): return lax.ppermute(shard, axis, pairs)]
  transfers between devices with their start and end apart: 8 -> 4, of which waited for: 6 -> 3; matrix products, arithmetic and copies ran while one was open for 19% -> 3% of each run, Pallas kernels for 0% -> 0%
where the time goes in v1:
time: 281 us; the launch traced here: 280 us
  waiting for transfers between devices  184 us (65%)
  Pallas kernels  23.6 us (8%)
  between operations  17.7 us (6%)
  blocking collectives  17.2 us (6%)
  local copies, waits for them, and re-layouts  14.9 us (5%)
  matrix products  11.9 us (4%)
  starting transfers between devices  5.08 us (2%)
  other arithmetic  4.93 us (2%)
    all_gather x1, waiting for transfers between devices, shards(): all_query_weight = lax.all_gather(query_weight, 'seq', axis=0, tiled=True)  132 us
    psum x1, waiting for transfers between devices, shards(): lax.psum(jnp.dot(gated, out_weight, preferred_element_type=jnp.float32),...  42.4 us
    pallas_call x1, Pallas kernels, delta(): pl.pallas_call(functools.partial(delta_kernel, count), out_shape=jax.Shap...  23.6 us
    all_gather x1, blocking collectives, shards(): lax.all_gather(kv_proj.astype(jnp.bfloat16), 'seq', axis=0, tiled=True)  17.2 us
    unnamed x34, local copies, waits for them, and re-layouts  10.5 us
    all_gather x1, waiting for transfers between devices, shards(): all_picked = lax.all_gather(picked, 'seq', axis=0, tiled=True)  9.37 us
    dot_general x1, matrix products, shards(): jnp.dot(normalized, all_query_weight, preferred_element_type=jnp.float32)  6.86 us
  transfers between devices with their start and end apart: 4, of which 3 were waited for; matrix products, arithmetic and copies ran while one was open for 3% of the time, Pallas kernels for 0%

profile of v1, /device:TPU:0, one launch (start us, length us, event | category | flops | bytes accessed | tf_op | source)
XLA Modules:
  0.0 279.7 jit_solution(17169358237753783862)
XLA Ops:
  8.0 0.7 slice.48
  8.8 0.7 slice.47
  10.2 5.0 %collective-permute-start = (bf16[3,2048]{1,0:T(4,128)(2,1)S(1)}, bf16[3,2048]{1,0:T(4,128)(2,1)S(1)}, u32[]{:S(2)}, u32[]{:S(2)}) collective-permute-start(bf16[3,2048]{1,0:T(4,128)(2,1)S(1)} %pad_maximum_fusion.1), channel_id=1, source_target_pairs={{0,4},{4,8},{8,12},{1,5},{5,9},{9,13},{2,6},{6,10},{10,14},{3,7},{... | collective-permute-start | bytes 36872 | tf_op jit(solution)/shard_map/ppermute | solution.py:236
  15.2 0.8 copy.30.beta_ref
  15.9 0.8 copy.31.decay_ref
  17.4 0.7 copy.32.rate_t_ref
  19.5 0.9 copy-done.2
  20.4 0.9 copy-done.3
  21.3 0.9 copy-done.4
  22.2 0.9 copy-done.5
  23.2 0.7 copy-done.6
  26.0 23.6 %delta_rule.1 = bf16[128,1024]{1,0:T(8,128)(2,1)S(1)} custom-call(bf16[128,512]{1,0:T(8,128)(2,1)S(1)} %copy-done.3, bf16[128,512]{1,0:T(8,128)(2,1)S(1)} %copy-done.4, bf16[128,1024]{1,0:T(8,128)(2,1)S(1)} %copy-done.2, bf16[128,1024]{1,0:T(8,128)(2,1)S(1)} %copy-done.5, f32[8,2048]{1,0:T(8,128)S(1)} %pad_convert_fusion.tail_ref, ...), custom_call_target="tpu_custom_call" | custom-call | flops 49999998976 | bytes 4000000 | tf_op jit(solution)/shard_map/delta_rule/pallas_call | solution.py:195
  49.6 1.7 fusion.38
  51.5 0.9 pad_maximum_fusion
  55.0 42.4 %all-reduce.3.cloned.1.call-done = f32[128,2048]{1,0:T(8,128)} async-done(((f32[128,2048]{1,0:T(8,128)}), f32[128,2048]{1,0:T(8,128)}) %all-reduce.3.cloned.1.call-update) | async-done | bytes 1048592 | tf_op jit(solution)/shard_map/psum | solution.py:299
  97.3 1.5 fusion.26
  98.8 9.4 %all-gather.5.cloned.1.call-done = bf16[2048,512]{1,0:T(8,128)(2,1)} async-done(((bf16[512,512]{1,0:T(8,128)(2,1)}), bf16[2048,512]{1,0:T(8,128)(2,1)}) %all-gather.5.cloned.1.call-update) | async-done | bytes 2097168 | tf_op jit(solution)/shard_map/all_gather | solution.py:283
  108.2 2.1 convolution_convert_fusion
  110.3 17.2 %all_gather.11 = bf16[512,512]{1,0:T(8,128)(2,1)S(1)} all-gather(bf16[128,512]{1,0:T(8,128)(2,1)S(1)} %convolution_convert_fusion), channel_id=1, replica_groups=mesh['groups'=2,'seq'=4,'head'=4] {'seq'}, dimensions={0}, use_global_device_ids=true | all-gather | bytes 655360 | tf_op jit(solution)/shard_map/all_gather | solution.py:326
  127.5 132.0 %all-gather.3.cloned.1.call-done = bf16[2048,2048]{1,0:T(8,128)(2,1)} async-done(((bf16[512,2048]{1,0:T(8,128)(2,1)}), bf16[2048,2048]{1,0:T(8,128)(2,1)}) %all-gather.3.cloned.1.call-update) | async-done | bytes 8388624 | tf_op jit(solution)/shard_map/all_gather | solution.py:281
  259.5 6.9 %fusion.32 = f32[128,2048]{0,1:T(8,128)S(1)} fusion(bf16[2048,2048]{1,0:T(8,128)(2,1)} %all-gather.3.cloned.1.call-done, bf16[128,2048]{1,0:T(8,128)(2,1)S(1)} %get-tuple-element.71, f32[2048]{0:T(1024)S(1)} %copy-done.14, f32[128]{0:T(128)S(1)} %add_rsqrt_fusion), kind=kOutput, calls=%fused_computation.49 | convolution fusion | flops 1074790400 | bytes 9970176 | tf_op jit(solution)/shard_map/dot_general | solution.py:303
  266.6 1.7 conditional.3
  268.7 1.7 conditional.2
  271.5 0.9 copy.40
  (65 shorter events, 10.4 us)
Async XLA Ops:
  8.0 89.3 %all-reduce.3.cloned.1.call-start = ((), (), s32[]{:S(2)}) async-start(), calls=%async_computation | async-start | bytes 2097152 | tf_op jit(solution)/shard_map/psum | solution.py:299
  10.2 7.9 %collective-permute-start = (bf16[3,2048]{1,0:T(4,128)(2,1)S(1)}, bf16[3,2048]{1,0:T(4,128)(2,1)S(1)}, u32[]{:S(2)}, u32[]{:S(2)}) collective-permute-start(bf16[3,2048]{1,0:T(4,128)(2,1)S(1)} %pad_maximum_fusion.1), channel_id=1, source_target_pairs={{0,4},{4,8},{8,12},{1,5},{5,9},{9,13},{2,6},{6,10},{10,14},{3,7},{... | collective-permute-start | bytes 36872 | tf_op jit(solution)/shard_map/ppermute | solution.py:236
  18.1 0.7 copy-start
  18.8 0.7 copy-start.1
  19.5 0.9 copy-start.2
  20.4 0.9 copy-start.3
  21.3 0.9 copy-start.4
  22.2 0.9 copy-start.5
  23.2 0.7 copy-start.6
  23.9 0.7 copy-start.7
  24.6 0.7 copy-start.8
  25.3 0.7 copy-start.9
  26.0 23.6 %copy-start.10 = (bf16[1024,2048]{1,0:T(8,128)(2,1)S(1)}, bf16[1024,2048]{1,0:T(8,128)(2,1)}, u32[]{:S(2)}) copy-start(bf16[1024,2048]{1,0:T(8,128)(2,1)} %param.34) | copy-start | bytes 12582916
  49.6 1.9 copy-start.13
  51.3 46.0 %copy-start.12 = (bf16[128,2048]{1,0:T(8,128)(2,1)S(1)}, bf16[128,2048]{1,0:T(8,128)(2,1)}, u32[]{:S(2)}) copy-start(bf16[128,2048]{1,0:T(8,128)(2,1)} %param.21) | copy-start | bytes 1572868
  51.3 56.8 %copy-start.14 = (f32[2048]{0:T(1024)S(1)}, f32[2048]{0:T(1024)}, u32[]{:S(2)}) copy-start(f32[2048]{0:T(1024)} %param.35) | copy-start | bytes 24580
  51.4 56.8 %all-gather.5.cloned.1.call-start = ((), (), s32[]{:S(2)}) async-start(), calls=%async_computation.2 | async-start | bytes 2621440 | tf_op jit(solution)/shard_map/all_gather | solution.py:283
  52.4 207.1 %all-gather.3.cloned.1.call-start = ((), (), s32[]{:S(2)}) async-start(), calls=%async_computation.1 | async-start | bytes 10485760 | tf_op jit(solution)/shard_map/all_gather | solution.py:281
  98.8 167.6 %copy-start.11 = (bf16[128,2048]{1,0:T(8,128)(2,1)}, bf16[128,2048]{1,0:T(8,128)(2,1)S(1)}, u32[]{:S(2)}) copy-start(bf16[128,2048]{1,0:T(8,128)(2,1)S(1)} %get-tuple-element.71) | copy-start | bytes 1572868
Sparse Core Ops, SparseCore 0:
  51.5 45.7 all-reduce.2
Sparse Core Ops, SparseCore 1:
  53.4 54.7 all-gather.4
  109.6 149.8 all-gather.2

commit v2 on v1

--- a/solution.py
+++ b/solution.py
@@ -29,6 +29,7 @@
 
 def delta_kernel(
     count,
+    groups,
     q_ref,
     k_ref,
     v_ref,
@@ -44,12 +45,19 @@
     rate_ref,
     rate_t_ref,
     gain_ref,
+    w_ref,
     out_ref,
+    full_ref,
     joined,
     enter,
     leave,
     send_sems,
     recv_sems,
+    own_sem,
+    z_send,
+    z_recv,
+    y_send,
+    y_recv,
 ):
     me = lax.axis_index("seq")
     rows = q_ref.shape[0]
@@ -60,7 +68,86 @@
 
     for peer in (lax.rem(me + 1, count), lax.rem(me + count - 1, count)):
         pl.semaphore_signal(barrier, inc=1, device_id={"seq": peer}, device_id_type=MESH)
-    pl.semaphore_wait(barrier, 2)
+    part = lax.axis_index("groups")
+    for e in range(1, groups):
+        pl.semaphore_signal(
+            barrier,
+            inc=1,
+            device_id={"groups": lax.rem(part + e, groups)},
+            device_id_type=MESH,
+        )
+    pl.semaphore_wait(barrier, 1 + groups)
+
+    depth = w_ref.shape[0]
+    piece = depth // groups
+
+    def rows_of(block, which):
+        return full_ref.at[pl.ds(pl.multiple_of(block * depth + which * piece, piece), piece)]
+
+    def inside(block):
+        return (block >= 0) & (block < count)
+
+    def clamp(block):
+        return jnp.clip(block, 0, count - 1)
+
+    def along(d, j):
+        sign = 1 if d == 0 else -1
+        block = clamp(me - sign * j)
+        source = w_ref.at[pl.ds(pl.multiple_of(part * piece, piece), piece)]
+        return pltpu.make_async_remote_copy(
+            src_ref=source if j == 0 else rows_of(block, part),
+            dst_ref=rows_of(block, part),
+            send_sem=z_send.at[d, j],
+            recv_sem=z_recv.at[d, j],
+            device_id={"seq": clamp(me + sign)},
+            device_id_type=MESH,
+        ), inside(me - sign * j) & inside(me + sign)
+
+    def landing(d, j):
+        sign = 1 if d == 0 else -1
+        block = clamp(me - sign * (j + 1))
+        return pltpu.make_async_remote_copy(
+            src_ref=rows_of(block, part),
+            dst_ref=rows_of(block, part),
+            send_sem=z_send.at[d, j],
+            recv_sem=z_recv.at[d, j],
+            device_id={"seq": clamp(me + sign)},
+            device_id_type=MESH,
+        ), inside(me - sign * (j + 1))
+
+    def across(e, d, j, which):
+        sign = 1 if d == 0 else -1
+        block = clamp(me - sign * (j + 1))
+        return pltpu.make_async_remote_copy(
+            src_ref=rows_of(block, which),
+            dst_ref=rows_of(block, which),
+            send_sem=y_send.at[e - 1, d, j],
+            recv_sem=y_recv.at[e - 1, d, j],
+            device_id={"groups": lax.rem(part + e, groups)},
+            device_id_type=MESH,
+        )
+
+    def relay(j):
+        for d in range(2):
+            copy, here = landing(d, j)
+
+            @pl.when(here)
+            def _():
+                copy.wait_recv()
+                for e in range(1, groups):
+                    across(e, d, j, part).start()
+
+            if j + 1 < count - 1:
+                onward, go = along(d, j + 1)
+                pl.when(go)(onward.start)
+
+    own = pltpu.make_async_copy(
+        w_ref, full_ref.at[pl.ds(pl.multiple_of(me * depth, depth), depth)], own_sem
+    )
+    for d in range(2):
+        first_copy, go = along(d, 0)
+        pl.when(go)(first_copy.start)
+    own.start()
 
     @pl.when(me == 0)
     def _():
@@ -148,6 +235,7 @@
         )
         injected.append(mm(stop, u, ((0,), (0,))))
 
+    relay(0)
     copies = []
     for h in range(value_heads):
         copy = pltpu.make_async_remote_copy(
@@ -182,27 +270,51 @@
         for copy in copies:
             copy.wait_send()
 
-
-def delta(count, q, k, v, gate, beta_logit, decay_logit, seq_length, cq, ck, cv, rate, gain):
+    for j in range(1, count - 1):
+        relay(j)
+    own.wait()
+    for j in range(count - 1):
+        for d in range(2):
+            sent, go = along(d, j)
+            pl.when(go)(sent.wait_send)
+            _, here = landing(d, j)
+
+            @pl.when(here)
+            def _():
+                for e in range(1, groups):
+                    across(e, d, j, part).wait_send()
+                    across(e, d, j, lax.rem(part + groups - e, groups)).wait_recv()
+
+
+def delta(count, weights, q, k, v, gate, beta_logit, decay_logit, seq_length, cq, ck, cv, rate, gain):
     rows, value_heads = beta_logit.shape
     width = q.shape[1] + k.shape[1] + v.shape[1]
     rim = rows - CONV + 1
+    groups = lax.axis_size("groups")
     tail = jnp.concatenate([q[rim:], k[rim:], v[rim:]], 1)
     tail = shifted(tail, "seq", 1).astype(jnp.float32)
     tail = jnp.concatenate([jnp.zeros((PAD - CONV + 1, width), jnp.float32), tail], 0)
     vmem = pl.BlockSpec(memory_space=pltpu.VMEM)
     smem = pl.BlockSpec(memory_space=pltpu.SMEM)
     return pl.pallas_call(
-        functools.partial(delta_kernel, count),
-        out_shape=jax.ShapeDtypeStruct(gate.shape, jnp.bfloat16),
-        in_specs=[vmem] * 8 + [smem] + [vmem] * 6,
-        out_specs=vmem,
+        functools.partial(delta_kernel, count, groups),
+        out_shape=(
+            jax.ShapeDtypeStruct(gate.shape, jnp.bfloat16),
+            jax.ShapeDtypeStruct((count * weights.shape[0], weights.shape[1]), jnp.bfloat16),
+        ),
+        in_specs=[vmem] * 8 + [smem] + [vmem] * 7,
+        out_specs=(vmem, pl.BlockSpec(memory_space=pl.ANY)),
         scratch_shapes=[
             pltpu.VMEM((rows + PAD, width), jnp.float32),
             pltpu.VMEM((value_heads, DK, DV), jnp.float32),
             pltpu.VMEM((value_heads, DK, DV), jnp.float32),
             pltpu.SemaphoreType.DMA((value_heads,)),
             pltpu.SemaphoreType.DMA((value_heads,)),
+            pltpu.SemaphoreType.DMA,
+            pltpu.SemaphoreType.DMA((2, count - 1)),
+            pltpu.SemaphoreType.DMA((2, count - 1)),
+            pltpu.SemaphoreType.DMA((groups - 1, 2, count - 1)),
+            pltpu.SemaphoreType.DMA((groups - 1, 2, count - 1)),
         ],
         compiler_params=pltpu.CompilerParams(
             collective_id=0, has_side_effects=True, vmem_limit_bytes=32 * 2**20
@@ -227,6 +339,7 @@
         rate[None, :],
         rate[:, None],
         gain[None, :],
+        weights,
     )
 
 
@@ -278,11 +391,10 @@
     seq_rank = lax.axis_index("seq")
     positions = seq_rank * row_count + jnp.arange(row_count, dtype=jnp.int32)
     length_now = seq_length[0]
-    all_query_weight = lax.all_gather(query_weight, "seq", axis=0, tiled=True)
-    picked = pick(key_value_weight, query_weight)
-    all_picked = lax.all_gather(picked, "seq", axis=0, tiled=True)
-    gated = delta(
+    weights = jnp.concatenate([query_weight, pick(key_value_weight, query_weight)], 1)
+    gated, all_weights = delta(
         lax.axis_size("seq"),
+        weights,
         query_in,
         key_in,
         value_in,
@@ -300,16 +412,9 @@
     hidden_out = (residual.astype(jnp.float32) + summed).astype(jnp.bfloat16)
     normalized = rms_scaled(hidden_out.astype(jnp.float32), attn_gain).astype(jnp.bfloat16)
     query_head_rows = query_weight.shape[1] // (2 * HEAD_WIDTH)
-    query_proj = jnp.dot(
-        normalized,
-        all_query_weight,
-        preferred_element_type=jnp.float32,
-    )
-    kv_proj = jnp.dot(
-        normalized,
-        all_picked,
-        preferred_element_type=jnp.float32,
-    )
+    projected = jnp.dot(normalized, all_weights, preferred_element_type=jnp.float32)
+    query_proj = projected[:, : query_weight.shape[1]]
+    kv_proj = projected[:, query_weight.shape[1] :]
     query_proj = query_proj.reshape(row_count, query_head_rows, 2, HEAD_WIDTH)
     queries_att = query_proj[:, :, 0].astype(jnp.bfloat16)
     gating_att = query_proj[:, :, 1]
@@ -334,7 +439,7 @@
         needed = jnp.logical_and(offset <= query_positions[-1], offset < length_now)
 
         def refresh(recurrent_state):
-            peak, _, _ = recurrent_state
+            peak, total, accum = recurrent_state
             scores = jnp.einsum(
                 "qhd,kd->hqk", block_queries, key_piece, preferred_element_type=jnp.float32
             ) * HEAD_WIDTH ** (-0.5)
@@ -392,7 +497,6 @@
         P("seq", "head"),
         P("seq", None),
     )
-
     return jax.shard_map(
         shards,
         mesh=mesh,

time: 281 us -> 231 us (0.82)
  waiting for transfers between devices: 184 us -> 39.6 us
  Pallas kernels: 23.6 us -> 125 us
  matrix products: 11.9 us -> 8.72 us
    all_gather x2 -> x0, waiting for transfers between devices: 141 us -> none  [the longest x1 132 us: shards(): all_query_weight = lax.all_gather(query_weight, 'seq', axis=0, tiled=True)]
    pallas_call x1, Pallas kernels: 23.6 us -> 125 us  [delta(): pl.pallas_call(functools.partial(delta_kernel, count, groups), out_shape=...]
    dot_general x2 -> x1, matrix products: 8.95 us -> 5.75 us  [shards(): jnp.dot(normalized, all_weights, preferred_element_type=jnp.float32)]
    unnamed x34 -> x36, local copies, waits for them, and re-layouts: 10.5 us -> 7.38 us
  transfers between devices with their start and end apart: 4 -> 2, of which waited for: 3 -> 1; matrix products, arithmetic and copies ran while one was open for 3% -> 2% of each run, Pallas kernels for 0% -> 0%
where the time goes in v2:
time: 231 us
  Pallas kernels  125 us (54%)
  waiting for transfers between devices  39.6 us (17%)
  between operations  16.3 us (7%)
  blocking collectives  15.5 us (7%)
  local copies, waits for them, and re-layouts  12.7 us (5%)
  matrix products  8.72 us (4%)
  other arithmetic  7.15 us (3%)
  starting transfers between devices  5.58 us (2%)
    pallas_call x1, Pallas kernels, delta(): pl.pallas_call(functools.partial(delta_kernel, count, groups), out_shape=...  125 us
    psum x1, waiting for transfers between devices, shards(): lax.psum(jnp.dot(gated, out_weight, preferred_element_type=jnp.float32),...  39.6 us
    all_gather x1, blocking collectives, shards(): lax.all_gather(kv_proj.astype(jnp.bfloat16), 'seq', axis=0, tiled=True)  15.5 us
    unnamed x36, local copies, waits for them, and re-layouts  7.38 us
    dot_general x1, matrix products, shards(): jnp.dot(normalized, all_weights, preferred_element_type=jnp.float32)  5.75 us
    ppermute x1, starting transfers between devices, shifted(): return lax.ppermute(shard, axis, pairs)  5.54 us
  transfers between devices with their start and end apart: 2, of which 1 were waited for; matrix products, arithmetic and copies ran while one was open for 2% of the time, Pallas kernels for 0%

profile of v2, /device:TPU:0, one launch (start us, length us, event | category | flops | bytes accessed | tf_op | source)
XLA Modules:
  0.0 230.6 jit_solution(18185394295972836157)
XLA Ops:
  7.3 0.9 slice.55
  8.2 0.7 slice.53
  8.9 0.7 slice.54
  9.6 0.6 pad_maximum_fusion.1
  10.2 5.5 %collective-permute-start = (bf16[3,2048]{1,0:T(4,128)(2,1)}, bf16[3,2048]{1,0:T(4,128)(2,1)}, u32[]{:S(2)}, u32[]{:S(2)}) collective-permute-start(bf16[3,2048]{1,0:T(4,128)(2,1)} %pad_maximum_fusion.1), channel_id=1, source_target_pairs={{0,4},{4,8},{8,12},{1,5},{5,9},{9,13},{2,6},{6,10},{10,14},{3,7},{... | collective-permute-start | bytes 36872 | tf_op jit(solution)/shard_map/ppermute | solution.py:349
  15.8 1.1 constant_dynamic-slice_fusion.1
  16.8 1.8 pad_maximum_fusion.w_ref
  19.6 0.7 pad_convert_fusion.tail_ref
  20.4 0.7 copy-done.7
  21.1 0.7 copy-done.8
  21.8 0.7 copy-done.9
  22.5 124.9 %delta_rule.1 = (bf16[128,1024]{1,0:T(8,128)(2,1)S(1)}, bf16[2048,2560]{1,0:T(8,128)(2,1)S(1)}) custom-call(bf16[128,512]{1,0:T(8,128)(2,1)S(1)} %copy-done.4, bf16[128,512]{1,0:T(8,128)(2,1)S(1)} %copy-done.5, bf16[128,1024]{1,0:T(8,128)(2,1)S(1)} %copy-done.3, bf16[128,1024]{1,0:T(8,128)(2,1)S(1)} %copy-done.6, f32[8,2048]{1,0:T(8,128)S(1)} %pad_convert_fusion.tail_ref, ...), custom_call_target="tpu_custom_call" | custom-call | flops 49999998976 | bytes 4000000 | tf_op jit(solution)/shard_map/delta_rule/pallas_call | solution.py:299
  147.4 4.0 %copy-done = bf16[2048,2560]{1,0:T(8,128)(2,1)} copy-done((bf16[2048,2560]{1,0:T(8,128)(2,1)}, bf16[2048,2560]{1,0:T(8,128)(2,1)S(1)}, u32[]{:S(2)}) %copy-start) | copy-done | bytes 10485784
  151.4 1.7 fusion.39
  153.1 0.6 fusion.38
  155.0 39.6 %all-reduce.3.cloned.1.call-done = f32[128,2048]{1,0:T(8,128)} async-done(((f32[128,2048]{1,0:T(8,128)}), f32[128,2048]{1,0:T(8,128)}) %all-reduce.3.cloned.1.call-update) | async-done | bytes 1048592 | tf_op jit(solution)/shard_map/psum | solution.py:411
  194.6 1.5 fusion.26
  196.1 5.7 %fusion.29 = f32[128,2560]{1,0:T(8,128)S(1)} fusion(bf16[2048,2560]{1,0:T(8,128)(2,1)} %copy-done, bf16[128,2048]{1,0:T(8,128)(2,1)S(1)} %get-tuple-element.75, f32[2048]{0:T(1024)S(1)} %copy-done.14, f32[128]{0:T(128)S(1)} %add_rsqrt_fusion), kind=kOutput, calls=%fused_computation.41 | convolution fusion | flops 1343225856 | bytes 12329472 | tf_op jit(solution)/shard_map/dot_general | solution.py:415
  202.6 15.5 %all_gather.3 = bf16[512,512]{1,0:T(8,128)(2,1)S(1)} all-gather(bf16[128,512]{1,0:T(8,128)(2,1)S(1)} %slice.78), channel_id=1, replica_groups=mesh['groups'=2,'seq'=4,'head'=4] {'seq'}, dimensions={0}, use_global_device_ids=true | all-gather | bytes 655360 | tf_op jit(solution)/shard_map/all_gather | solution.py:431
  218.1 1.7 conditional.2
  218.1 0.7 broadcast_compare_fusion
  220.1 1.7 conditional.3
  220.1 0.7 broadcast_compare_fusion.1
  222.9 0.9 copy.40
  (63 shorter events, 4.4 us)
Async XLA Ops:
  7.2 13.1 %copy-start.3 = (bf16[128,1024]{1,0:T(8,128)(2,1)S(1)}, bf16[128,1024]{1,0:T(8,128)(2,1)}, u32[]{:S(2)}) copy-start(bf16[128,1024]{1,0:T(8,128)(2,1)} %v_ref.1) | copy-start | bytes 786436
  7.2 13.1 %copy-start.4 = (bf16[128,512]{1,0:T(8,128)(2,1)S(1)}, bf16[128,512]{1,0:T(8,128)(2,1)}, u32[]{:S(2)}) copy-start(bf16[128,512]{1,0:T(8,128)(2,1)} %q_ref.1) | copy-start | bytes 393220
  7.2 13.1 %copy-start.5 = (bf16[128,512]{1,0:T(8,128)(2,1)S(1)}, bf16[128,512]{1,0:T(8,128)(2,1)}, u32[]{:S(2)}) copy-start(bf16[128,512]{1,0:T(8,128)(2,1)} %k_ref.1) | copy-start | bytes 393220
  7.2 12.1 %copy-start.15 = (f32[128,8]{0,1:T(8,128)S(1)}, f32[128,8]{0,1:T(8,128)}, u32[]{:S(2)}) copy-start(f32[128,8]{0,1:T(8,128)} %param.26) | copy-start | bytes 12292
  7.2 12.2 %copy-start.1 = (f32[128,8]{0,1:T(8,128)S(1)}, f32[128,8]{0,1:T(8,128)}, u32[]{:S(2)}) copy-start(f32[128,8]{0,1:T(8,128)} %param.27) | copy-start | bytes 12292
  7.2 12.3 %copy-start.2 = (f32[8]{0:T(128)S(1)}, f32[8]{0:T(128)}, u32[]{:S(2)}) copy-start(f32[8]{0:T(128)} %param.32) | copy-start | bytes 100
  7.2 13.1 %copy-start.10 = (f32[128]{0:T(128)S(1)}, f32[128]{0:T(128)}, u32[]{:S(2)}) copy-start(f32[128]{0:T(128)} %param.33) | copy-start | bytes 1540
  7.2 13.1 %copy-start.6 = (bf16[128,1024]{1,0:T(8,128)(2,1)S(1)}, bf16[128,1024]{1,0:T(8,128)(2,1)}, u32[]{:S(2)}) copy-start(bf16[128,1024]{1,0:T(8,128)(2,1)} %gate_ref.1) | copy-start | bytes 786436
  7.2 187.4 %all-reduce.3.cloned.1.call-start = ((), (), s32[]{:S(2)}) async-start(), calls=%async_computation | async-start | bytes 2097152 | tf_op jit(solution)/shard_map/psum | solution.py:411
  10.2 9.4 %collective-permute-start = (bf16[3,2048]{1,0:T(4,128)(2,1)}, bf16[3,2048]{1,0:T(4,128)(2,1)}, u32[]{:S(2)}, u32[]{:S(2)}) collective-permute-start(bf16[3,2048]{1,0:T(4,128)(2,1)} %pad_maximum_fusion.1), channel_id=1, source_target_pairs={{0,4},{4,8},{8,12},{1,5},{5,9},{9,13},{2,6},{6,10},{10,14},{3,7},{... | collective-permute-start | bytes 36872 | tf_op jit(solution)/shard_map/ppermute | solution.py:349
  20.4 0.7 copy-start.7
  21.1 0.7 copy-start.8
  21.8 0.7 copy-start.9
  22.5 128.9 %copy-start.11 = (bf16[1024,2048]{1,0:T(8,128)(2,1)S(1)}, bf16[1024,2048]{1,0:T(8,128)(2,1)}, u32[]{:S(2)}) copy-start(bf16[1024,2048]{1,0:T(8,128)(2,1)} %param.34) | copy-start | bytes 12582916
  147.4 4.0 %copy-start = (bf16[2048,2560]{1,0:T(8,128)(2,1)}, bf16[2048,2560]{1,0:T(8,128)(2,1)S(1)}, u32[]{:S(2)}) copy-start(bf16[2048,2560]{1,0:T(8,128)(2,1)S(1)} %get-tuple-element.53) | copy-start | bytes 31457284
  151.4 43.3 %copy-start.13 = (bf16[128,2048]{1,0:T(8,128)(2,1)S(1)}, bf16[128,2048]{1,0:T(8,128)(2,1)}, u32[]{:S(2)}) copy-start(bf16[128,2048]{1,0:T(8,128)(2,1)} %param.21) | copy-start | bytes 1572868
  151.4 44.7 %copy-start.14 = (f32[2048]{0:T(1024)S(1)}, f32[2048]{0:T(1024)}, u32[]{:S(2)}) copy-start(f32[2048]{0:T(1024)} %param.35) | copy-start | bytes 24580
  196.1 5.8 %copy-start.12 = (bf16[128,2048]{1,0:T(8,128)(2,1)}, bf16[128,2048]{1,0:T(8,128)(2,1)S(1)}, u32[]{:S(2)}) copy-start(bf16[128,2048]{1,0:T(8,128)(2,1)S(1)} %get-tuple-element.75) | copy-start | bytes 1572868
Sparse Core Ops, SparseCore 0:
  153.2 41.3 all-reduce.2
